TPU v7x, 32 devices: a whole 2x2x4 slice. The times are simulated.
32 devices in a mesh: car: 2 (over y), branch: 4 (over x, core), pts: 4 (over z).
Axes of the slice: x: 2, y: 2, z: 4, core: 2. Of those that a mesh axis runs over, the one named last changes fastest.
Arguments:
- anchors: bfloat16 [512, 384], P(('car', 'branch', 'pts')), parts along dimension 0, may hold values from -6 to 6
- queries: bfloat16 [4096, 384], P(('car', 'branch', 'pts')), parts along dimension 0, may hold values from -6 to 6
- query_kind: int32 [4096], P(('car', 'branch', 'pts')), parts along dimension 0, may hold values from 0 to 1
- live_count: int32 [32], P(('car', 'branch', 'pts')), parts along dimension 0, may hold values from 16 to 128, as said below
- anchor_gain: float32 [384], replicated, may hold values from 0.25 to 1.75
- query_gain: float32 [384], replicated, may hold values from 0.25 to 1.75
- w_query: bfloat16 [384, 384], replicated, may hold values from -0.3125 to 0.3125
- w_key: bfloat16 [384, 384], replicated, may hold values from -0.3125 to 0.3125
- w_value: bfloat16 [384, 384], replicated, may hold values from -0.3125 to 0.3125
- w_out: bfloat16 [384, 384], replicated, may hold values from -0.3125 to 0.3125
- cotangent: bfloat16 [4096, 384], P(('car', 'branch', 'pts')), parts along dimension 0, may hold values from -6 to 6
Outputs:
- fields: bfloat16 [4096, 384], P(('car', 'branch', 'pts')), parts along dimension 0
- query_grad: float32 [4096, 384], P(('car', 'branch', 'pts')), parts along dimension 0
- anchor_grad: float32 [512, 384], P(('car', 'branch', 'pts')), parts along dimension 0
There are 2 independent parts, one for each index of `car`. A program takes and returns all parts, laid end to end along the dimension named above; an argument that names none is the same for every part. Nothing has to cross between parts.
Inputs may be any that keep to these rules, and one draw needn't show every extreme that they name: `live_count`: each entry counts used slots of one device's 128 slots, the used ones first; some device has all 128 used in every draw.
All inputs are finite; a program needn't handle non-finite values.
Results may differ from a plain program's by a relative error of at most 0.011.
Values may be sent and summed in bfloat16 or wider, within the bound.
A program may use at most 64 MiB of HBM per device.

v0:
```python
import functools

import jax
import jax.numpy as jnp
from jax import lax
from jax.experimental import pallas as pl
from jax.experimental.pallas import tpu as pltpu
from jax.sharding import PartitionSpec as P

HEADS = 6
MESH = pl.DeviceIdType.MESH
F32 = jnp.float32
BF16 = jnp.bfloat16


def nn(a, b):
    return lax.dot_general(a, b, (((1,), (0,)), ((), ())), preferred_element_type=F32)


def nt(a, b):
    return lax.dot_general(a, b, (((1,), (1,)), ((), ())), preferred_element_type=F32)


def unit_rows(rows):
    values = rows.astype(F32)
    center = values - jnp.mean(values, axis=-1, keepdims=True)
    inverse = lax.rsqrt(jnp.mean(center * center, axis=-1, keepdims=True) + 1e-05)
    return center * inverse, inverse


def norm_back(unit, inverse, gain, grad):
    scaled = grad * gain
    first = jnp.mean(scaled, axis=-1, keepdims=True)
    second = jnp.mean(scaled * unit, axis=-1, keepdims=True)
    return inverse * (scaled - first - unit * second)


def kernel(
    n_branch,
    n_pts,
    anchors_in,
    queries_in,
    kind_in,
    live_in,
    again_in,
    qgain_in,
    wq_in,
    wk_in,
    wv_in,
    wo_in,
    cot_in,
    fields,
    qgrad,
    agrad,
    gathered,
    outgoing,
    incoming,
    own,
    queries,
    kind,
    live_count,
    again,
    qgain,
    wq,
    wk,
    wv,
    wo,
    cot,
    wk_t,
    wv_t,
    q_pairs,
    g_pairs,
    load_sem,
    gather_send,
    gather_recv,
    reduce_send,
    reduce_recv,
):
    block, width = anchors_in.shape
    rows = queries_in.shape[0]
    head = width // HEADS
    pair = 2 * head
    n_pairs = HEADS // 2
    scale = 1.0 / head**0.5
    half_branch = n_branch // 2
    half_blocks = half_branch * n_pts
    b = lax.axis_index("branch")
    p = lax.axis_index("pts")
    side = lax.div(b, half_branch)
    b_in = lax.rem(b, half_branch)
    place = b_in * n_pts + p

    def peers(other):
        found = []
        for dp in range(n_pts):
            for db in range(half_branch):
                if other or dp or db:
                    pb = lax.rem(b_in + db, half_branch)
                    pp = lax.rem(p + dp, n_pts)
                    pside = 1 - side if other else side
                    found.append((pside, pb, pp))
        return found

    def device(peer):
        return {"branch": peer[0] * half_branch + peer[1], "pts": peer[2]}

    def at_place(where):
        return pl.ds(pl.multiple_of(where * block, block), block)

    def gain_row(gain):
        return gain[...].reshape(1, width)

    barrier = pltpu.get_barrier_semaphore()
    mine, others = peers(False), peers(True)
    for peer in mine + others:
        pl.semaphore_signal(barrier, inc=1, device_id=device(peer), device_id_type=MESH)

    own_rows = gathered.at[side, at_place(place)]
    pairs = [
        (anchors_in, own_rows),
        (queries_in, queries),
        (qgain_in, qgain),
        (wq_in, wq),
        (cot_in, cot),
        (live_in, live_count),
        (wo_in, wo),
        (wk_in, wk),
        (wv_in, wv),
        (again_in, again),
        (kind_in, kind),
    ]
    loads = [
        pltpu.make_async_copy(src, dst, load_sem.at[i]) for i, (src, dst) in enumerate(pairs)
    ]
    for load in loads:
        load.start()
    loads[0].wait()
    pl.semaphore_wait(barrier, len(mine) + len(others))

    for which, group in enumerate((mine, others)):
        for peer in group:
            pltpu.make_async_remote_copy(
                src_ref=own_rows,
                dst_ref=own_rows,
                send_sem=gather_send.at[which],
                recv_sem=gather_recv.at[which],
                device_id=device(peer),
                device_id_type=MESH,
            ).start()

    for load in loads[1:7]:
        load.wait()
    live = (lax.broadcasted_iota(jnp.int32, (rows, 1), 0) < live_count[0]).astype(F32)
    q_unit, q_inverse = unit_rows(queries[...])
    q_heads = nn((q_unit * gain_row(qgain)).astype(BF16), wq[...]).astype(BF16)
    q_heads = (q_heads.astype(F32) * scale).astype(BF16)
    grad_rows = (cot[...].astype(F32) * live).astype(BF16)
    grad_mixed = nt(grad_rows, wo[...]).astype(BF16)
    low = lax.broadcasted_iota(jnp.int32, (rows, pair), 1) < head
    for i in range(n_pairs):
        cols = slice(i * pair, (i + 1) * pair)
        for source, target in ((q_heads, q_pairs), (grad_mixed, g_pairs)):
            part = source[:, cols].astype(F32)
            target[i, :rows, :] = jnp.where(low, part, 0.0).astype(BF16)
            target[i, rows:, :] = jnp.where(low, 0.0, part).astype(BF16)
    for load in loads[7:]:
        load.wait()
    wk_t[...] = wk[...].T
    wv_t[...] = wv[...].T
    is_volume = (kind[...] == 1).astype(jnp.int32)

    def attend(at_side):
        unit, _ = unit_rows(gathered[at_side])
        normed = (unit * gain_row(again)).astype(BF16)
        keys = nn(normed, wk[...]).astype(BF16)
        values = nn(normed, wv[...]).astype(BF16)
        keys_t = nt(wk_t[...], normed).astype(BF16)
        values_t = nt(wv_t[...], normed).astype(BF16)
        allowed = (is_volume == at_side).astype(F32)
        allowed = jnp.concatenate([allowed, allowed], axis=1)
        mixed_t, gq_t, gk, gv = [], [], [], []
        for i in range(n_pairs):
            cols = slice(i * pair, (i + 1) * pair)
            scores = nt(keys[:, cols], q_pairs[i])
            grad_probs = nt(values[:, cols], g_pairs[i])
            expo = jnp.exp(scores - jnp.max(scores, axis=0, keepdims=True))
            probs = expo * (allowed / jnp.sum(expo, axis=0, keepdims=True))
            probs_low = probs.astype(BF16)
            delta = jnp.sum(grad_probs * probs, axis=0, keepdims=True)
            grad_scores = (probs * (grad_probs - delta)).astype(BF16)
            both = nn(values_t[cols, :], probs_low)
            mixed_t += [both[:head, :rows], both[head:, rows:]]
            both = nn(keys_t[cols, :], grad_scores)
            gq_t += [both[:head, :rows], both[head:, rows:]]
            gk.append(nn(grad_scores, q_pairs[i]).astype(BF16))
            gv.append(nn(probs_low, g_pairs[i]).astype(BF16))
        projected = nn(jnp.concatenate(gk, axis=1), wk_t[...])
        projected = projected + nn(jnp.concatenate(gv, axis=1), wv_t[...])
        outgoing[at_side] = projected.astype(BF16)
        return jnp.concatenate(mixed_t, axis=0), jnp.concatenate(gq_t, axis=0)

    def arrived(buffer, count, send, recv):
        return pltpu.make_async_remote_copy(
            src_ref=buffer.at[0, pl.ds(0, count * block)],
            dst_ref=buffer.at[0, pl.ds(0, count * block)],
            send_sem=send,
            recv_sem=recv,
            device_id=device(others[0]),
            device_id_type=MESH,
        )

    def give(group, which):
        for peer in group:
            pltpu.make_async_remote_copy(
                src_ref=outgoing.at[peer[0], at_place(peer[1] * n_pts + peer[2])],
                dst_ref=incoming.at[side, at_place(place)],
                send_sem=reduce_send.at[which],
                recv_sem=reduce_recv.at[which],
                device_id=device(peer),
                device_id_type=MESH,
            ).start()

    arrived(gathered, len(mine), gather_send.at[0], gather_recv.at[0]).wait_recv()
    mixed_a, gq_a = attend(side)
    give(mine, 0)
    own[...] = outgoing[side, at_place(place), :].astype(F32)
    arrived(gathered, len(others), gather_send.at[1], gather_recv.at[1]).wait_recv()
    mixed_b, gq_b = attend(1 - side)
    give(others, 1)

    mixed = (mixed_a + mixed_b).T.astype(BF16)
    residual = queries[...].astype(F32) + nn(mixed, wo[...])
    fields[...] = (live * residual).astype(BF16)
    grad_queries = ((gq_a + gq_b) * scale).T.astype(BF16)
    grad_normed = nt(grad_queries, wq[...])
    q_unit, q_inverse = unit_rows(queries[...])
    back = norm_back(q_unit, q_inverse, gain_row(qgain), grad_normed)
    qgrad[...] = live * (cot[...].astype(F32) + back)

    a_unit, a_inverse = unit_rows(gathered[side, at_place(place), :])
    incoming[side, at_place(place), :] = jnp.zeros((block, width), BF16)
    arrived(incoming, len(mine), reduce_send.at[0], reduce_recv.at[0]).wait_recv()
    arrived(incoming, len(others), reduce_send.at[1], reduce_recv.at[1]).wait_recv()
    total = own[...]
    for s in range(2):
        for i in range(half_blocks):
            total = total + incoming[s, i * block : (i + 1) * block, :].astype(F32)
    agrad[...] = norm_back(a_unit, a_inverse, gain_row(again), total)
    arrived(gathered, len(mine), gather_send.at[0], gather_recv.at[0]).wait_send()
    arrived(gathered, len(others), gather_send.at[1], gather_recv.at[1]).wait_send()
    arrived(outgoing, len(mine), reduce_send.at[0], reduce_recv.at[0]).wait_send()
    arrived(outgoing, len(others), reduce_send.at[1], reduce_recv.at[1]).wait_send()


def store_results(*refs):
    copies = [
        pltpu.make_async_copy(refs[i], refs[3 + i], refs[6].at[i]) for i in range(3)
    ]
    for copy in copies:
        copy.start()
    for copy in copies:
        copy.wait()


def on_device(n_branch, n_pts, *arrays):
    (anchors, queries, kind, live, again, qgain, wq, wk, wv, wo, cot) = arrays
    block, width = anchors.shape
    rows = queries.shape[0]
    half_rows = block * n_branch * n_pts // 2
    pair = 2 * (width // HEADS)
    vmem = pltpu.VMEM
    dma = pltpu.SemaphoreType.DMA
    square = (width, width)
    shapes = (
        vmem((rows, width), BF16),
        vmem((rows, width), F32),
        vmem((block, width), F32),
    )
    results = pl.pallas_call(
        functools.partial(kernel, n_branch, n_pts),
        out_shape=shapes,
        in_specs=[pl.BlockSpec(memory_space=pltpu.HBM)] * 11,
        out_specs=[pl.BlockSpec(memory_space=pltpu.VMEM)] * 3,
        scratch_shapes=[
            vmem((2, half_rows, width), BF16),
            vmem((2, half_rows, width), BF16),
            vmem((2, half_rows, width), BF16),
            vmem((block, width), F32),
            vmem((rows, width), BF16),
            vmem((1, rows), jnp.int32),
            pltpu.SMEM((1,), jnp.int32),
            vmem((width,), F32),
            vmem((width,), F32),
            vmem(square, BF16),
            vmem(square, BF16),
            vmem(square, BF16),
            vmem(square, BF16),
            vmem((rows, width), BF16),
            vmem(square, BF16),
            vmem(square, BF16),
            vmem((HEADS // 2, 2 * rows, pair), BF16),
            vmem((HEADS // 2, 2 * rows, pair), BF16),
            dma((11,)),
            dma((2,)),
            dma((2,)),
            dma((2,)),
            dma((2,)),
        ],
        compiler_params=pltpu.CompilerParams(
            collective_id=0, has_side_effects=True
        ),
    )(
        anchors,
        queries,
        kind.reshape(1, rows),
        live,
        again,
        qgain,
        wq,
        wk,
        wv,
        wo,
        cot,
    )
    return pl.pallas_call(
        store_results,
        out_shape=tuple(jax.ShapeDtypeStruct(x.shape, x.dtype) for x in shapes),
        in_specs=[pl.BlockSpec(memory_space=pltpu.VMEM)] * 3,
        out_specs=[pl.BlockSpec(memory_space=pltpu.HBM)] * 3,
        scratch_shapes=[dma((3,))],
    )(*[pltpu.with_memory_space_constraint(x, pltpu.VMEM) for x in results])


def solution(mesh):
    spread = P(("car", "branch", "pts"), None)
    flat = P(("car", "branch", "pts"))
    return jax.shard_map(
        functools.partial(on_device, mesh.shape["branch"], mesh.shape["pts"]),
        mesh=mesh,
        in_specs=(spread, spread, flat, flat) + (P(),) * 6 + (spread,),
        out_specs=(spread, spread, spread),
        check_vma=False,
    )
```

profile of v0, /device:TPU:0, one launch (start us, length us, event | category | flops | bytes accessed | tf_op | source)
XLA Modules:
  0.0 20.9 jit_solution(811100345146775688)
XLA Ops:
  1.3 18.8 %shard_map.130 = (bf16[128,384]{1,0:T(8,128)(2,1)S(1)}, f32[128,384]{1,0:T(8,128)S(1)}, f32[16,384]{1,0:T(8,128)S(1)}) custom-call(bf16[16,384]{1,0:T(8,128)(2,1)} %anchors_in.1, bf16[128,384]{1,0:T(8,128)(2,1)} %queries_in.1, s32[1,128]{1,0:T(1,128)} %bitcast.1, s32[1]{0:T(128)S(6)} %copy.14.live_in, f32[384]{0:T(512)} %again_in.1, f32[384]{0:T(512)} %qgain_in.1, ...), custom_call_target="tpu_custom_call" | custom-call | tf_op jit(solution)/shard_map/pallas_call | solution.py:279
  20.1 0.7 %shard_map.131 = (bf16[128,384]{1,0:T(8,128)(2,1)}, f32[128,384]{1,0:T(8,128)}, f32[16,384]{1,0:T(8,128)}) custom-call(bf16[128,384]{1,0:T(8,128)(2,1)S(1)} %get-tuple-element.6.refs_0_, f32[128,384]{1,0:T(8,128)S(1)} %get-tuple-element.7.refs_1_, f32[16,384]{1,0:T(8,128)S(1)} %get-tuple-element.8.refs_2_), custom_call_target="tpu_custom_call" | custom-call | tf_op jit(solution)/shard_map/pallas_call | solution.py:325
where the time goes:
time: 21.1 us; the launch traced here: 20.9 us
  Pallas kernels  19.6 us (93%)
  between operations  1.29 us (6%)
    pallas_call x1, Pallas kernels, on_device(): pl.pallas_call(functools.partial(kernel, n_branch, n_pts), out_shape=shap...  18.8 us
    pallas_call x1, Pallas kernels, on_device(): pl.pallas_call(store_results, out_shape=tuple((jax.ShapeDtypeStruct(x.sha...  0.74 us

commit v1 on v0

v1 whole, which is shorter than its diff:
```python
import functools

import jax
import jax.numpy as jnp
from jax import lax
from jax.experimental import pallas as pl
from jax.experimental.pallas import tpu as pltpu
from jax.sharding import PartitionSpec as P

HEADS = 6
MESH = pl.DeviceIdType.MESH
F32 = jnp.float32
BF16 = jnp.bfloat16


def nn(a, b):
    return lax.dot_general(a, b, (((1,), (0,)), ((), ())), preferred_element_type=F32)


def nt(a, b):
    return lax.dot_general(a, b, (((1,), (1,)), ((), ())), preferred_element_type=F32)


def unit_rows(rows):
    values = rows.astype(F32)
    center = values - jnp.mean(values, axis=-1, keepdims=True)
    inverse = lax.rsqrt(jnp.mean(center * center, axis=-1, keepdims=True) + 1e-05)
    return center * inverse, inverse


def norm_back(unit, inverse, gain, grad):
    scaled = grad * gain
    first = jnp.mean(scaled, axis=-1, keepdims=True)
    second = jnp.mean(scaled * unit, axis=-1, keepdims=True)
    return inverse * (scaled - first - unit * second)


def kernel(
    n_branch,
    n_pts,
    anchors_in,
    queries_in,
    kind_in,
    live_in,
    again_in,
    qgain_in,
    wq_in,
    wk_in,
    wv_in,
    wo_in,
    cot_in,
    fields,
    qgrad,
    agrad,
    anchors,
    own_norm,
    gathered,
    outgoing,
    incoming,
    queries,
    kind,
    live_count,
    again,
    qgain,
    wq,
    wk,
    wv,
    wo,
    cot,
    wk_t,
    wv_t,
    sides,
    asked,
    key_query,
    value_grad,
    probs_low,
    grad_scores,
    answers,
    load_sem,
    gather_send,
    gather_recv,
    reduce_send,
    reduce_recv,
    pair_send,
    pair_recv,
):
    block, width = anchors_in.shape
    rows = queries_in.shape[0]
    head = width // HEADS
    pair = 2 * head
    n_pairs = HEADS // 2
    scale = 1.0 / head**0.5
    half_branch = n_branch // 2
    half_blocks = half_branch * n_pts
    b = lax.axis_index("branch")
    p = lax.axis_index("pts")
    side = lax.div(b, half_branch)
    b_in = lax.rem(b, half_branch)
    couple = lax.div(b, 2)
    handled = lax.rem(b, 2)
    place = b_in * n_pts + p
    handler_place = couple * n_pts + p
    partner = {"branch": couple * 2 + 1 - handled, "pts": p}
    far = p < n_pts // 2

    def at_place(where):
        return pl.ds(pl.multiple_of(where * block, block), block)

    def gain_row(gain):
        return gain[...].reshape(1, width)

    def pts_order():
        return [jnp.where(far, n_pts - 1 - i, i) for i in range(n_pts)]

    barrier = pltpu.get_barrier_semaphore()
    for dp in range(n_pts):
        for db in range(n_branch):
            if dp or db:
                pl.semaphore_signal(
                    barrier,
                    inc=1,
                    device_id={
                        "branch": lax.rem(b + db, n_branch),
                        "pts": lax.rem(p + dp, n_pts),
                    },
                    device_id_type=MESH,
                )

    pairs = [
        (anchors_in, anchors),
        (again_in, again),
        (queries_in, queries),
        (qgain_in, qgain),
        (wq_in, wq),
        (cot_in, cot),
        (live_in, live_count),
        (wo_in, wo),
        (kind_in, kind),
        (wk_in, wk),
        (wv_in, wv),
    ]
    loads = [
        pltpu.make_async_copy(src, dst, load_sem.at[i])
        for i, (src, dst) in enumerate(pairs)
    ]
    for load in loads:
        load.start()
    for load in loads[:2]:
        load.wait()
    a_unit, a_inverse = unit_rows(anchors[...])
    own_norm[...] = (a_unit * gain_row(again)).astype(BF16)
    pl.semaphore_wait(barrier, n_branch * n_pts - 1)

    def send_or_keep(source, target, b_to, p_to, send, recv):
        mine = (b_to == b) & (p_to == p)

        @pl.when(mine)
        def _():
            pltpu.make_async_copy(source, target, recv).start()

        @pl.when(jnp.logical_not(mine))
        def _():
            pltpu.make_async_remote_copy(
                src_ref=source,
                dst_ref=target,
                send_sem=send,
                recv_sem=recv,
                device_id={"branch": b_to, "pts": p_to},
                device_id_type=MESH,
            ).start()

    for p_to in pts_order():
        for i in range(half_branch):
            b_to = lax.rem(couple + 1 + i, half_branch) * 2 + side
            send_or_keep(
                own_norm,
                gathered.at[at_place(place)],
                b_to,
                p_to,
                gather_send,
                gather_recv,
            )

    def to_partner(source, target, i):
        return pltpu.make_async_remote_copy(
            src_ref=source,
            dst_ref=target,
            send_sem=pair_send.at[i],
            recv_sem=pair_recv.at[i],
            device_id=partner,
            device_id_type=MESH,
        )

    for load in loads[2:9]:
        load.wait()
    live = (lax.broadcasted_iota(jnp.int32, (rows, 1), 0) < live_count[0]).astype(F32)
    q_unit, q_inverse = unit_rows(queries[...])
    q_heads = nn((q_unit * gain_row(qgain)).astype(BF16), wq[...]).astype(BF16)
    asked[0, 0] = (q_heads.astype(F32) * scale).astype(BF16)
    grad_rows = (cot[...].astype(F32) * live).astype(BF16)
    asked[0, 1] = nt(grad_rows, wo[...]).astype(BF16)
    sides[0] = jnp.broadcast_to((kind[...] == 1).astype(F32), sides.shape[1:])
    ask = to_partner(asked.at[0], asked.at[1], 0)
    ask.start()
    ask_side = to_partner(sides.at[0], sides.at[1], 1)
    ask_side.start()

    low = lax.broadcasted_iota(jnp.int32, (rows, pair), 1) < head

    def products(j):
        for i in range(n_pairs):
            cols = slice(i * pair, (i + 1) * pair)
            for which, weights, result in ((0, wk, key_query), (1, wv, value_grad)):
                part = asked[j, which, :, cols].astype(F32)
                both = jnp.concatenate(
                    [jnp.where(low, part, 0.0), jnp.where(low, 0.0, part)], axis=0
                ).astype(BF16)
                result[j * n_pairs + i] = nt(weights[:, cols], both).astype(BF16)

    for load in loads[9:]:
        load.wait()
    products(0)
    ask.wait()
    ask_side.wait()
    products(1)
    wk_t[...] = wk[...].T
    wv_t[...] = wv[...].T

    def arrived(buffer, count, send, recv):
        return pltpu.make_async_remote_copy(
            src_ref=buffer.at[pl.ds(0, count * block)],
            dst_ref=buffer.at[pl.ds(0, count * block)],
            send_sem=send,
            recv_sem=recv,
            device_id=partner,
            device_id_type=MESH,
        )

    arrived(gathered, half_blocks, gather_send, gather_recv).wait_recv()
    normed = gathered[...]
    handled_f = handled.astype(F32)
    total = None
    for t in range(2 * n_pairs):
        matches = (sides[t // n_pairs, :1, :] == handled_f).astype(F32)
        allowed = jnp.concatenate([matches, matches], axis=1)
        scores = nn(normed, key_query[t])
        grad_probs = nn(normed, value_grad[t])
        expo = jnp.exp(scores - jnp.max(scores, axis=0, keepdims=True))
        probs = expo * (allowed / jnp.sum(expo, axis=0, keepdims=True))
        delta = jnp.sum(grad_probs * probs, axis=0, keepdims=True)
        p_low = probs.astype(BF16)
        g_low = (probs * (grad_probs - delta)).astype(BF16)
        probs_low[t] = p_low
        grad_scores[t] = g_low
        part = nt(g_low, key_query[t]) + nt(p_low, value_grad[t])
        total = part if total is None else total + part
    outgoing[...] = total.astype(BF16)
    for p_to in pts_order():
        for i in range(half_branch):
            j = lax.rem(b_in + 1 + i, half_branch)
            send_or_keep(
                outgoing.at[at_place(j * n_pts + p_to)],
                incoming.at[at_place(handler_place)],
                handled * half_branch + j,
                p_to,
                reduce_send,
                reduce_recv,
            )

    keys_t = nt(wk_t[...], normed).astype(BF16)
    values_t = nt(wv_t[...], normed).astype(BF16)
    for j in (1, 0):
        for i in range(n_pairs):
            cols = slice(i * pair, (i + 1) * pair)
            t = j * n_pairs + i
            for which, left, right in (
                (0, values_t, probs_low),
                (1, keys_t, grad_scores),
            ):
                both = nn(left[cols, :], right[t]).astype(BF16)
                answers[j, which, i * pair : i * pair + head, :] = both[:head, :rows]
                answers[j, which, i * pair + head : (i + 1) * pair, :] = both[head:, rows:]
        if j == 1:
            answer = to_partner(answers.at[1], answers.at[2], 2)
            answer.start()
    answer.wait()
    mixed = (answers[0, 0].astype(F32) + answers[2, 0].astype(F32)).T.astype(BF16)
    residual = queries[...].astype(F32) + nn(mixed, wo[...])
    fields[...] = (live * residual).astype(BF16)
    grad_queries = (answers[0, 1].astype(F32) + answers[2, 1].astype(F32)) * scale
    grad_normed = nt(grad_queries.T.astype(BF16), wq[...])
    q_unit, q_inverse = unit_rows(queries[...])
    back = norm_back(q_unit, q_inverse, gain_row(qgain), grad_normed)
    qgrad[...] = live * (cot[...].astype(F32) + back)

    kept = side == handled
    for buffer, send in ((gathered, gather_send), (outgoing, reduce_send)):
        arrived(buffer, half_blocks - 1, send, gather_recv).wait_send()

        @pl.when(jnp.logical_not(kept))
        def _():
            arrived(buffer, 1, send, gather_recv).wait_send()

    a_unit, a_inverse = unit_rows(anchors[...])
    arrived(incoming, half_blocks, reduce_send, reduce_recv).wait_recv()
    total = incoming[:block, :].astype(F32)
    for i in range(1, half_blocks):
        total = total + incoming[i * block : (i + 1) * block, :].astype(F32)
    agrad[...] = norm_back(a_unit, a_inverse, gain_row(again), total)


def store_results(*refs):
    copies = [
        pltpu.make_async_copy(refs[i], refs[3 + i], refs[6].at[i]) for i in range(3)
    ]
    for copy in copies:
        copy.start()
    for copy in copies:
        copy.wait()


def on_device(n_branch, n_pts, *arrays):
    (anchors, queries, kind, live, again, qgain, wq, wk, wv, wo, cot) = arrays
    block, width = anchors.shape
    rows = queries.shape[0]
    half_rows = block * n_branch * n_pts // 2
    pair = 2 * (width // HEADS)
    tiles = HEADS
    vmem = pltpu.VMEM
    dma = pltpu.SemaphoreType.DMA
    square = (width, width)
    shapes = (
        vmem((rows, width), BF16),
        vmem((rows, width), F32),
        vmem((block, width), F32),
    )
    results = pl.pallas_call(
        functools.partial(kernel, n_branch, n_pts),
        out_shape=shapes,
        in_specs=[pl.BlockSpec(memory_space=pltpu.HBM)] * 11,
        out_specs=[pl.BlockSpec(memory_space=pltpu.VMEM)] * 3,
        scratch_shapes=[
            vmem((block, width), BF16),
            vmem((block, width), BF16),
            vmem((half_rows, width), BF16),
            vmem((half_rows, width), BF16),
            vmem((half_rows, width), BF16),
            vmem((rows, width), BF16),
            vmem((1, rows), jnp.int32),
            pltpu.SMEM((1,), jnp.int32),
            vmem((width,), F32),
            vmem((width,), F32),
            vmem(square, BF16),
            vmem(square, BF16),
            vmem(square, BF16),
            vmem(square, BF16),
            vmem((rows, width), BF16),
            vmem(square, BF16),
            vmem(square, BF16),
            vmem((2, 8, rows), F32),
            vmem((2, 2, rows, width), BF16),
            vmem((tiles, width, 2 * rows), BF16),
            vmem((tiles, width, 2 * rows), BF16),
            vmem((tiles, half_rows, 2 * rows), BF16),
            vmem((tiles, half_rows, 2 * rows), BF16),
            vmem((3, 2, width, rows), BF16),
            dma((11,)),
            dma,
            dma,
            dma,
            dma,
            dma((3,)),
            dma((3,)),
        ],
        compiler_params=pltpu.CompilerParams(
            collective_id=0, has_side_effects=True
        ),
    )(
        anchors,
        queries,
        kind.reshape(1, rows),
        live,
        again,
        qgain,
        wq,
        wk,
        wv,
        wo,
        cot,
    )
    return pl.pallas_call(
        store_results,
        out_shape=tuple(jax.ShapeDtypeStruct(x.shape, x.dtype) for x in shapes),
        in_specs=[pl.BlockSpec(memory_space=pltpu.VMEM)] * 3,
        out_specs=[pl.BlockSpec(memory_space=pltpu.HBM)] * 3,
        scratch_shapes=[dma((3,))],
    )(*[pltpu.with_memory_space_constraint(x, pltpu.VMEM) for x in results])


def solution(mesh):
    spread = P(("car", "branch", "pts"), None)
    flat = P(("car", "branch", "pts"))
    return jax.shard_map(
        functools.partial(on_device, mesh.shape["branch"], mesh.shape["pts"]),
        mesh=mesh,
        in_specs=(spread, spread, flat, flat) + (P(),) * 6 + (spread,),
        out_specs=(spread, spread, spread),
        check_vma=False,
    )
```

time: 21.1 us -> 19.2 us (0.910)
  Pallas kernels: 19.6 us -> 17.6 us
    pallas_call x1, Pallas kernels: 18.8 us -> 16.9 us  [on_device(): pl.pallas_call(functools.partial(kernel, n_branch, n_pts), out_shape=shap...]
where the time goes in v1:
time: 19.2 us; the launch traced here: 18.9 us
  Pallas kernels  17.6 us (92%)
  between operations  1.29 us (7%)
    pallas_call x1, Pallas kernels, on_device(): pl.pallas_call(functools.partial(kernel, n_branch, n_pts), out_shape=shap...  16.9 us
    pallas_call x1, Pallas kernels, on_device(): pl.pallas_call(store_results, out_shape=tuple((jax.ShapeDtypeStruct(x.sha...  0.74 us

profile of v1, /device:TPU:0, one launch (start us, length us, event | category | flops | bytes accessed | tf_op | source)
XLA Modules:
  0.0 18.9 jit_solution(12832176589061510863)
XLA Ops:
  1.3 16.9 %shard_map.130 = (bf16[128,384]{1,0:T(8,128)(2,1)S(1)}, f32[128,384]{1,0:T(8,128)S(1)}, f32[16,384]{1,0:T(8,128)S(1)}) custom-call(bf16[16,384]{1,0:T(8,128)(2,1)} %anchors_in.1, bf16[128,384]{1,0:T(8,128)(2,1)} %queries_in.1, s32[1,128]{1,0:T(1,128)} %bitcast.1, s32[1]{0:T(128)S(6)} %copy.14.live_in, f32[384]{0:T(512)} %again_in.1, f32[384]{0:T(512)} %qgain_in.1, ...), custom_call_target="tpu_custom_call" | custom-call | tf_op jit(solution)/shard_map/pallas_call | solution.py:337
  18.2 0.7 %shard_map.131 = (bf16[128,384]{1,0:T(8,128)(2,1)}, f32[128,384]{1,0:T(8,128)}, f32[16,384]{1,0:T(8,128)}) custom-call(bf16[128,384]{1,0:T(8,128)(2,1)S(1)} %get-tuple-element.6.refs_0_, f32[128,384]{1,0:T(8,128)S(1)} %get-tuple-element.7.refs_1_, f32[16,384]{1,0:T(8,128)S(1)} %get-tuple-element.8.refs_2_), custom_call_target="tpu_custom_call" | custom-call | tf_op jit(solution)/shard_map/pallas_call | solution.py:391
